TPU v7x, 32 devices: a whole 2x2x4 slice. The times are simulated.
32 devices in a mesh: gx: 4 (over x, core), gy: 4 (over z), gz: 2 (over y).
Axes of the slice: x: 2, y: 2, z: 4, core: 2. Of those that a mesh axis runs over, the one named last changes fastest.
Arguments:
- relative_placements: float32 [3, 12, 12, 8, 128], P(None, 'gx', 'gy', 'gz'), may hold values from 0 to 1
- mass_per_density: float32 [12, 12, 8, 128], P('gx', 'gy', 'gz'), may hold values from 0.004 to 0.04
- opening_heat_level: float32 [12, 12, 8, 128], P('gx', 'gy', 'gz'), may hold values from 0.5 to 2
- bin_fill_counts: int32 [12, 12, 8], P('gx', 'gy', 'gz'), may hold values from 16 to 128
Outputs:
- final_temp: float32 [12, 12, 8, 128], P('gx', 'gy', 'gz')
Inputs may be any that keep to these rules, and one draw needn't show every extreme that they name: Tile cell t holds particles in slots 0 to bin_fill_counts[t] - 1; the other slots are empty and are no source.
All inputs are finite; a program needn't handle non-finite values.
Results may differ from a plain program's by a relative error of at most 0.0003.
Values sent between devices are 32-bit elements; how exact they have to be, the bound alone decides.
A program may use at most 64 MiB of HBM per device.

v0:
```python
import jax
import jax.numpy as jnp
from jax import lax
from jax.sharding import PartitionSpec as P

step_factor = 2.0


def shifted(block, axis, distance):
    devices = range(lax.axis_size(axis))
    route = [((i - distance) % len(devices), i) for i in devices]
    return lax.ppermute(block, axis, route)


def with_halo(value, sides, width):
    for axis, dim in sides:
        size, length = (lax.axis_size(axis), value.shape[dim])
        up = [(i, (i + 1) % size) for i in range(size)]
        down = [(j, i) for i, j in up]
        last = lax.slice_in_dim(value, length - width, length, axis=dim)
        leading = lax.slice_in_dim(value, 0, width, axis=dim)
        before = lax.ppermute(last, axis, up)
        after = lax.ppermute(leading, axis, down)
        value = jnp.concatenate([before, value, after], axis=dim)
    return value


def paired(fields, periodic_enclosure):
    extent_x, extent_y, extent_z = periodic_enclosure
    bin_dimensions = fields.shape[-1]
    forward = [(0, 0, 0)] + [
        (sx, sy, sz)
        for sx in (-1, 0, 1)
        for sy in (-1, 0, 1)
        for sz in (-1, 0, 1)
        if (sx, sy, sz) > (0, 0, 0)
    ]

    def visit(column, totals):
        col_x = column // extent_y
        col_y = column % extent_y

        def column_at(shift_x, shift_y):
            column_part = lax.dynamic_slice_in_dim(fields, col_x + 1 + shift_x, 1, 1)
            column_part = lax.dynamic_slice_in_dim(column_part, col_y + 1 + shift_y, 1, 2)
            return column_part[:, 0, 0]

        target = column_at(0, 0)[:, 1 : 1 + extent_z]
        own_part = jnp.zeros((2, extent_z, bin_dimensions), jnp.float32)
        for shift_x, shift_y, shift_z in forward:
            source = column_at(shift_x, shift_y)[:, 1 + shift_z : 1 + shift_z + extent_z]
            dist_sq = (float(shift_x) + source[0][:, None, :] - target[0][:, :, None]) ** 2
            dist_sq = (
                dist_sq + (float(shift_y) + source[1][:, None, :] - target[1][:, :, None]) ** 2
            )
            dist_sq = (
                dist_sq + (float(shift_z) + source[2][:, None, :] - target[2][:, :, None]) ** 2
            )
            kernel = jnp.maximum(1.0 - jnp.sqrt(dist_sq), 0.0) ** 3
            shared = kernel * (target[5][:, :, None] + source[5][:, None, :])
            spread = source[4][:, None, :] - target[4][:, :, None]
            toward_target = shared * source[3][:, None, :]
            own_part = own_part + jnp.stack(
                [jnp.sum(toward_target * spread, axis=2), jnp.sum(toward_target, axis=2)]
            )
            if (shift_x, shift_y, shift_z) != (0, 0, 0):
                toward_source = shared * target[3][:, :, None]
                returned = jnp.stack(
                    [-jnp.sum(toward_source * spread, axis=1), jnp.sum(toward_source, axis=1)]
                )
                corner = (0, col_x + 1 + shift_x, col_y + 1 + shift_y, 1 + shift_z, 0)
                window = lax.dynamic_slice(totals, corner, (2, 1, 1, extent_z, bin_dimensions))
                totals = lax.dynamic_update_slice(
                    totals, window + returned.reshape((2, 1, 1, extent_z, bin_dimensions)), corner
                )
        corner = (0, col_x + 1, col_y + 1, 1, 0)
        window = lax.dynamic_slice(totals, corner, (2, 1, 1, extent_z, bin_dimensions))
        return lax.dynamic_update_slice(
            totals, window + own_part.reshape((2, 1, 1, extent_z, bin_dimensions)), corner
        )

    totals = jnp.zeros((2, extent_x + 2, extent_y + 2, extent_z + 2, bin_dimensions), jnp.float32)
    return lax.fori_loop(0, extent_x * extent_y, visit, totals)


def fold_back(totals):
    for shift_by in (1, -1):
        rim = totals[:, -1] if shift_by == 1 else totals[:, 0]
        arrived = shifted(rim, "gx", shift_by)
        if shift_by == 1:
            totals = totals.at[:, 1].add(arrived)
        else:
            totals = totals.at[:, -2].add(arrived)
    totals = totals[:, 1:-1]
    for shift_by in (1, -1):
        rim = totals[:, :, -1] if shift_by == 1 else totals[:, :, 0]
        arrived = shifted(rim, "gy", shift_by)
        if shift_by == 1:
            totals = totals.at[:, :, 1].add(arrived)
        else:
            totals = totals.at[:, :, -2].add(arrived)
    totals = totals[:, :, 1:-1]
    for shift_by in (1, -1):
        rim = totals[:, :, :, -1] if shift_by == 1 else totals[:, :, :, 0]
        arrived = shifted(rim, "gz", shift_by)
        if shift_by == 1:
            totals = totals.at[:, :, :, 1].add(arrived)
        else:
            totals = totals.at[:, :, :, -2].add(arrived)
    totals = totals[:, :, :, 1:-1]
    return (totals[0], totals[1])


def with_temp(fields, temp):
    return jnp.concatenate([fields[:4], temp[None], fields[5:6]], axis=0)


def step_size(row_sums):
    largest = lax.pmax(jnp.max(row_sums), ("gx", "gy", "gz"))
    return step_factor / largest


def section_halo(temp):
    return with_halo(temp, (("gx", 0), ("gy", 1), ("gz", 2)), 1)


def local(relative_placements, mass_per_density, opening_heat_level, bin_fill_counts):
    bin_dimensions = opening_heat_level.shape[-1]
    occupied = (
        jnp.arange(bin_dimensions, dtype=jnp.int32)[None, None, None, :]
        < bin_fill_counts[..., None]
    ).astype(jnp.float32)
    smoothed_particle_measure = mass_per_density * occupied
    layered_buffers = jnp.concatenate(
        [relative_placements, smoothed_particle_measure[None], opening_heat_level[None]], axis=0
    )
    periodic_enclosure = opening_heat_level.shape[:3]
    near = with_halo(layered_buffers, (("gx", 1), ("gy", 2), ("gz", 3)), 1)
    fields = jnp.concatenate([near, (near[4] ** 2.5)[None]], axis=0)

    def flows(section_fields):
        return fold_back(paired(section_fields, periodic_enclosure))

    reference_heat_rate, row_sums = flows(fields)
    super_interval_length = step_size(row_sums * occupied)
    leading_subset = opening_heat_level + 2.0 / 15.0 * super_interval_length * reference_heat_rate
    initial_flow, unused_one = flows(with_temp(fields, section_halo(leading_subset)))
    second = (
        1.5 * leading_subset
        - 0.5 * opening_heat_level
        + 0.6 * super_interval_length * initial_flow
        - 0.4 * super_interval_length * reference_heat_rate
    )
    flow_second, unused_two = flows(with_temp(fields, section_halo(second)))
    final_temp = (
        25.0 / 12.0 * second
        - 5.0 / 6.0 * leading_subset
        - 0.25 * opening_heat_level
        + 5.0 / 6.0 * super_interval_length * flow_second
        - 5.0 / 9.0 * super_interval_length * reference_heat_rate
    )
    return final_temp


def solution(mesh):
    in_specs = (
        P(None, "gx", "gy", "gz", None),
        P("gx", "gy", "gz", None),
        P("gx", "gy", "gz", None),
        P("gx", "gy", "gz"),
    )
    out_specs = P("gx", "gy", "gz", None)
    return jax.shard_map(local, mesh=mesh, in_specs=in_specs, out_specs=out_specs, check_vma=False)
```

profile of v0, /device:TPU:0, one launch (start us, length us, event | category | flops | bytes accessed | tf_op | source)
XLA Modules:
  0.0 387.4 jit_solution(11387767187985435500)
XLA Ops:
  5.8 2.3 collective-permute-start.2
  8.1 2.1 collective-permute-start.3
  10.2 2.1 collective-permute-done.2
  15.9 2.7 collective-permute-done.4
  20.0 77.0 %while.72 = (s32[]{:T(128)}, f32[2,5,5,6,128]{4,3,0,2,1:T(8,128)S(1)}, f32[6,5,5,6,128]{4,3,0,2,1:T(8,128)S(1)}, s32[]{:T(128)}, s32[]{:T(128)}, /*index=5*/s32[...) while((s32[]{:T(128)}, f32[2,5,5,6,128]{4,3,0,2,1:T(8,128)S(1)}, ...), condition=%wide.region_55.56_spmd, body=%wide.region_0.55_spmd.sunk | while | flops 21871652 | bytes 1245886 | solution.py:83
  97.2 3.3 collective-permute-done.6
  103.4 4.4 %collective-permute-done.8 = f32[2,3,6,128]{3,0,2,1:T(2,128)S(1)} collective-permute-done((f32[2,3,6,128]{3,0,2,1:T(2,128)S(1)}, f32[2,3,6,128]{3,0,2,1:T(2,128)S(1)}, u32[]{:S(2)}, u32[]{:S(2)}) %collective-permute-start.8) | collective-permute-done | bytes 18464 | tf_op jit(solution)/shard_map/ppermute | solution.py:12
  108.8 2.8 collective-permute-done.9
  112.9 2.5 collective-permute-done.10
  116.7 2.5 collective-permute-done.11
  119.9 38.4 %pmax.7 = f32[]{:T(128)} all-reduce(f32[]{:T(128)} %select_reduce_fusion), channel_id=1, replica_groups=mesh['gx'=4,'gy'=4,'gz'=2] {'gx','gy','gz'}, use_global_device_ids=true, to_apply=%region_57.58 | all-reduce | flops 1 | bytes 8 | tf_op jit(solution)/shard_map/pmax | solution.py:119
  162.2 2.2 collective-permute-start.14
  168.0 2.5 collective-permute-start.16
  174.4 77.1 %while.73 = (s32[]{:T(128)}, f32[2,5,5,6,128]{4,3,0,2,1:T(8,128)S(1)}, f32[6,5,5,6,128]{4,3,0,2,1:T(8,128)S(1)}, s32[]{:T(128)}, s32[]{:T(128)}, /*index=5*/s32[...) while((s32[]{:T(128)}, ...), condition=%wide.region_113.114_spmd, body=%wide.region_58.113_spmd.sunk | while | flops 21871652 | bytes 1245886 | solution.py:83
  251.6 3.4 collective-permute-done.18
  258.2 4.2 %collective-permute-done.20 = f32[2,3,6,128]{3,2,1,0:T(8,128)S(1)} collective-permute-done((f32[2,3,6,128]{3,2,1,0:T(8,128)S(1)}, f32[2,3,6,128]{3,2,1,0:T(8,128)S(1)}, u32[]{:S(2)}, u32[]{:S(2)}) %collective-permute-start.20) | collective-permute-done | bytes 18464 | tf_op jit(solution)/shard_map/ppermute | solution.py:12
  264.2 2.1 collective-permute-done.21
  266.6 3.5 collective-permute-done.22
  270.4 3.5 collective-permute-done.23
  277.2 3.8 collective-permute-start.27
  286.8 77.2 %while.74 = (s32[]{:T(128)}, f32[2,5,5,6,128]{4,3,0,2,1:T(8,128)S(1)}, f32[6,5,5,6,128]{4,3,0,2,1:T(8,128)S(1)}, s32[]{:T(128)}, s32[]{:T(128)}, /*index=5*/s32[...) while((s32[]{:T(128)}, ...), condition=%wide.region_169.170_spmd, body=%wide.region_114.169_spmd.sunk | while | flops 21871652 | bytes 1245886 | solution.py:83
  364.1 3.4 collective-permute-done.30
  370.2 4.8 %collective-permute-done.32 = f32[2,3,6,128]{3,2,1,0:T(8,128)S(1)} collective-permute-done((f32[2,3,6,128]{3,2,1,0:T(8,128)S(1)}, f32[2,3,6,128]{3,2,1,0:T(8,128)S(1)}, u32[]{:S(2)}, u32[]{:S(2)}) %collective-permute-start.32) | collective-permute-done | bytes 18464 | tf_op jit(solution)/shard_map/ppermute | solution.py:12
  375.0 2.1 collective-permute-start.33
  (1328 shorter events, 278.2 us)
Async XLA Ops:
  1.6 4.0 %collective-permute-start = (f32[5,1,3,4,128]{4,3,0,2,1:T(4,128)S(1)}, f32[5,1,3,4,128]{4,3,0,2,1:T(4,128)S(1)}, u32[]{:S(2)}, u32[]{:S(2)}) collective-permute-start(f32[5,1,3,4,128]{4,3,0,2,1:T(4,128)S(1)} %get-tuple-element.1266), channel_id=1, source_target_pairs={{0,8},{8,16},{16,24},{24,0},{1,9},{9,17},{17,25},{25,1},{2,10},{10... | collective-permute-start | bytes 92168 | tf_op jit(solution)/shard_map/ppermute | solution.py:22
  5.8 6.5 %collective-permute-start.2 = (f32[5,5,1,4,128]{4,3,0,2,1:T(4,128)S(1)}, f32[5,5,1,4,128]{4,3,0,2,1:T(4,128)S(1)}, u32[]{:S(2)}, u32[]{:S(2)}) collective-permute-start(f32[5,5,1,4,128]{4,3,0,2,1:T(4,128)S(1)} %get-tuple-element.1264), channel_id=1, source_target_pairs={{0,2},{2,4},{4,6},{6,0},{1,3},{3,5},{5,7},{7,1},{8,10},{10,12},{12... | collective-permute-start | bytes 153608 | tf_op jit(solution)/shard_map/ppermute | solution.py:22
  8.1 5.6 %collective-permute-start.3 = (f32[5,5,1,4,128]{4,3,0,2,1:T(4,128)S(1)}, f32[5,5,1,4,128]{4,3,0,2,1:T(4,128)S(1)}, u32[]{:S(2)}, u32[]{:S(2)}) collective-permute-start(f32[5,5,1,4,128]{4,3,0,2,1:T(4,128)S(1)} %get-tuple-element.1265), channel_id=1, source_target_pairs={{2,0},{4,2},{6,4},{0,6},{3,1},{5,3},{7,5},{1,7},{10,8},{12,10},{14... | collective-permute-start | bytes 153608 | tf_op jit(solution)/shard_map/ppermute | solution.py:23
  13.9 4.8 %collective-permute-start.4 = (f32[5,5,5,1,128]{4,3,0,2,1:T(1,128)S(1)}, f32[5,5,5,1,128]{4,3,0,2,1:T(1,128)S(1)}, u32[]{:S(2)}, u32[]{:S(2)}) collective-permute-start(f32[5,5,5,1,128]{4,3,0,2,1:T(1,128)S(1)} %get-tuple-element.1262), channel_id=1, source_target_pairs={{0,1},{1,0},{2,3},{3,2},{4,5},{5,4},{6,7},{7,6},{8,9},{9,8},{10,11... | collective-permute-start | bytes 192008 | tf_op jit(solution)/shard_map/ppermute | solution.py:22
  15.2 4.3 %collective-permute-start.5 = (f32[5,5,5,1,128]{4,3,0,2,1:T(1,128)S(1)}, f32[5,5,5,1,128]{4,3,0,2,1:T(1,128)S(1)}, u32[]{:S(2)}, u32[]{:S(2)}) collective-permute-start(f32[5,5,5,1,128]{4,3,0,2,1:T(1,128)S(1)} %get-tuple-element.1263), channel_id=1, source_target_pairs={{1,0},{0,1},{3,2},{2,3},{5,4},{4,5},{7,6},{6,7},{9,8},{8,9},{11,10... | collective-permute-start | bytes 192008 | tf_op jit(solution)/shard_map/ppermute | solution.py:23
  102.2 5.6 %collective-permute-start.8 = (f32[2,3,6,128]{3,0,2,1:T(2,128)S(1)}, f32[2,3,6,128]{3,0,2,1:T(2,128)S(1)}, u32[]{:S(2)}, u32[]{:S(2)}) collective-permute-start(f32[2,3,6,128]{3,0,2,1:T(2,128)S(1)} %slice_bitcast_fusion.187), channel_id=1, source_target_pairs={{6,0},{0,2},{2,4},{4,6},{7,1},{1,3},{3,5},{5,7},{14,8},{8,10},{10,... | collective-permute-start | bytes 55304 | tf_op jit(solution)/shard_map/ppermute | solution.py:12
  107.8 3.8 collective-permute-start.9
  111.7 3.7 collective-permute-start.10
  115.4 3.7 collective-permute-start.11
  162.2 5.5 %collective-permute-start.14 = (f32[5,1,4,128]{3,2,0,1:T(4,128)S(1)}, f32[5,1,4,128]{3,2,0,1:T(4,128)S(1)}, u32[]{:S(2)}, u32[]{:S(2)}) collective-permute-start(f32[5,1,4,128]{3,2,0,1:T(4,128)S(1)} %get-tuple-element.1276), channel_id=1, source_target_pairs={{0,2},{2,4},{4,6},{6,0},{1,3},{3,5},{5,7},{7,1},{8,10},{10,12},{12... | collective-permute-start | bytes 30728 | tf_op jit(solution)/shard_map/ppermute | solution.py:22
  168.0 4.2 %collective-permute-start.16 = (f32[5,5,1,128]{3,2,0,1:T(1,128)S(1)}, f32[5,5,1,128]{3,2,0,1:T(1,128)S(1)}, u32[]{:S(2)}, u32[]{:S(2)}) collective-permute-start(f32[5,5,1,128]{3,2,0,1:T(1,128)S(1)} %get-tuple-element.1272), channel_id=1, source_target_pairs={{0,1},{1,0},{2,3},{3,2},{4,5},{5,4},{6,7},{7,6},{8,9},{9,8},{10,11... | collective-permute-start | bytes 38408 | tf_op jit(solution)/shard_map/ppermute | solution.py:22
  170.5 3.7 collective-permute-start.17
  256.8 5.7 %collective-permute-start.20 = (f32[2,3,6,128]{3,2,1,0:T(8,128)S(1)}, f32[2,3,6,128]{3,2,1,0:T(8,128)S(1)}, u32[]{:S(2)}, u32[]{:S(2)}) collective-permute-start(f32[2,3,6,128]{3,2,1,0:T(8,128)S(1)} %slice_bitcast_fusion.184), channel_id=1, source_target_pairs={{6,0},{0,2},{2,4},{4,6},{7,1},{1,3},{3,5},{5,7},{14,8},{8,10},{10,... | collective-permute-start | bytes 55304 | tf_op jit(solution)/shard_map/ppermute | solution.py:12
  262.4 3.9 %collective-permute-start.21 = (f32[2,3,6,128]{3,2,1,0:T(8,128)S(1)}, f32[2,3,6,128]{3,2,1,0:T(8,128)S(1)}, u32[]{:S(2)}, u32[]{:S(2)}) collective-permute-start(f32[2,3,6,128]{3,2,1,0:T(8,128)S(1)} %slice_bitcast_fusion.183), channel_id=1, source_target_pairs={{2,0},{4,2},{6,4},{0,6},{3,1},{5,3},{7,5},{1,7},{10,8},{12,10},{14... | collective-permute-start | bytes 55304 | tf_op jit(solution)/shard_map/ppermute | solution.py:12
  266.4 3.7 collective-permute-start.22
  270.2 3.7 collective-permute-start.23
  277.2 5.5 %collective-permute-start.26 = (f32[5,1,4,128]{3,2,0,1:T(4,128)S(1)}, f32[5,1,4,128]{3,2,0,1:T(4,128)S(1)}, u32[]{:S(2)}, u32[]{:S(2)}) collective-permute-start(f32[5,1,4,128]{3,2,0,1:T(4,128)S(1)} %get-tuple-element.1274), channel_id=1, source_target_pairs={{0,2},{2,4},{4,6},{6,0},{1,3},{3,5},{5,7},{7,1},{8,10},{10,12},{12... | collective-permute-start | bytes 30728 | tf_op jit(solution)/shard_map/ppermute | solution.py:22
  277.2 5.5 %collective-permute-start.27 = (f32[5,1,4,128]{3,2,0,1:T(4,128)S(1)}, f32[5,1,4,128]{3,2,0,1:T(4,128)S(1)}, u32[]{:S(2)}, u32[]{:S(2)}) collective-permute-start(f32[5,1,4,128]{3,2,0,1:T(4,128)S(1)} %get-tuple-element.1275), channel_id=1, source_target_pairs={{2,0},{4,2},{6,4},{0,6},{3,1},{5,3},{7,5},{1,7},{10,8},{12,10},{14... | collective-permute-start | bytes 30728 | tf_op jit(solution)/shard_map/ppermute | solution.py:23
  282.7 3.8 collective-permute-start.28
  282.9 3.7 collective-permute-start.29
  369.3 5.7 %collective-permute-start.32 = (f32[2,3,6,128]{3,2,1,0:T(8,128)S(1)}, f32[2,3,6,128]{3,2,1,0:T(8,128)S(1)}, u32[]{:S(2)}, u32[]{:S(2)}) collective-permute-start(f32[2,3,6,128]{3,2,1,0:T(8,128)S(1)} %slice_bitcast_fusion.181), channel_id=1, source_target_pairs={{6,0},{0,2},{2,4},{4,6},{7,1},{1,3},{3,5},{5,7},{14,8},{8,10},{10,... | collective-permute-start | bytes 55304 | tf_op jit(solution)/shard_map/ppermute | solution.py:12
  375.0 4.1 %collective-permute-start.33 = (f32[2,3,6,128]{3,2,1,0:T(8,128)S(1)}, f32[2,3,6,128]{3,2,1,0:T(8,128)S(1)}, u32[]{:S(2)}, u32[]{:S(2)}) collective-permute-start(f32[2,3,6,128]{3,2,1,0:T(8,128)S(1)} %slice_bitcast_fusion.180), channel_id=1, source_target_pairs={{2,0},{4,2},{6,4},{0,6},{3,1},{5,3},{7,5},{1,7},{10,8},{12,10},{14... | collective-permute-start | bytes 55304 | tf_op jit(solution)/shard_map/ppermute | solution.py:12
  379.1 3.7 collective-permute-start.34
  383.0 3.7 collective-permute-start.35
  (15 other events, 50.2 us)
where the time goes:
time: 388 us; the launch traced here: 387 us
  other arithmetic  190 us (49%)
  waiting for transfers between devices  72 us (19%)
  starting transfers between devices  39.9 us (10%)
  blocking collectives  38.4 us (10%)
  local copies, waits for them, and re-layouts  36.3 us (9%)
  loops' own time  9.42 us (2%)
    reduce_sum x189, other arithmetic, visit(): jnp.sum(toward_target * spread, axis=2)  178 us
    ppermute x18, waiting for transfers between devices, shifted(): return lax.ppermute(block, axis, route)  51.4 us
    pmax x1, blocking collectives, step_size(): largest = lax.pmax(jnp.max(row_sums), ('gx', 'gy', 'gz'))  38.4 us
    dynamic_update_slice x243, local copies, waits for them, and re-layouts, visit(): lax.dynamic_update_slice(totals, window + returned.reshape((2, 1, 1, exte...  30.3 us
    ppermute x9, starting transfers between devices, with_halo(): after = lax.ppermute(leading, axis, down)  15.7 us
    ppermute x9, waiting for transfers between devices, with_halo(): before = lax.ppermute(last, axis, up)  15.5 us
    ppermute x18, starting transfers between devices, shifted(): return lax.ppermute(block, axis, route)  14.9 us
    another operation x3, loops' own time, paired(): return lax.fori_loop(0, extent_x * extent_y, visit, totals)  9.42 us
  transfers between devices with their start and end apart: 36, of which 33 were waited for; matrix products, arithmetic and copies ran while one was open for 0% of the time, Pallas kernels for 0%

commit v1 on v0

v1 whole, which is shorter than its diff:
```python
import functools
import itertools
import jax
import jax.numpy as jnp
from jax import lax
from jax.experimental import pallas as pl
from jax.experimental.pallas import tpu as pltpu
from jax.sharding import PartitionSpec as P

AXES = ("gx", "gy", "gz")
MESH = pl.DeviceIdType.MESH
f32, bf16 = jnp.float32, jnp.bfloat16
DIRS = [d for d in itertools.product((-1, 0, 1), repeat=3) if d != (0, 0, 0)]
COLUMNS = [(ex, ey) for ex in (-1, 0, 1) for ey in (-1, 0, 1)]


def split3(tile):
    hi = tile.astype(bf16).astype(f32)
    rest = tile - hi
    mid = rest.astype(bf16).astype(f32)
    return hi, mid, rest - mid


def kernel(dims, block, f_in, out, f_all, k_all, bt, at, w_all, u1, u2, mx, mx_parts, fsend, frecv, usend, urecv, msend, mrecv):
    bx, by, bz = block
    lanes = f_in.shape[-1]
    me = [lax.axis_index(a) for a in AXES]
    row = lax.broadcasted_iota(jnp.int32, (8, lanes), 0)

    def neighbour(d):
        return tuple(lax.rem(me[k] + (d[k] + dims[k]), dims[k]) if d[k] else me[k] for k in range(3))

    def peer(axis, hop):
        return tuple(lax.rem(me[k] + hop, dims[k]) if k == axis else me[k] for k in range(3))

    barrier = pltpu.get_barrier_semaphore()
    count = 0
    for d in DIRS:
        pl.semaphore_signal(barrier, inc=1, device_id=neighbour(d), device_id_type=MESH)
        count += 1
    for axis in range(3):
        for hop in range(1, dims[axis]):
            pl.semaphore_signal(barrier, inc=1, device_id=peer(axis, hop), device_id_type=MESH)
            count += 1
    pl.semaphore_wait(barrier, count)

    def piece(d, base):
        src, dst = [], []
        for k in range(3):
            n = block[k]
            if d[k] == 0:
                src.append(pl.ds(base, n))
                dst.append(pl.ds(1, n))
            elif d[k] == 1:
                src.append(pl.ds(base + n - 1, 1))
                dst.append(pl.ds(0, 1))
            else:
                src.append(pl.ds(base, 1))
                dst.append(pl.ds(n + 1, 1))
        return tuple(src), tuple(dst)

    def halo_copies(src_ref, base, dst_ref, ssem, rsem):
        copies = []
        for i, d in enumerate(DIRS):
            src, dst = piece(d, base)
            copies.append(
                pltpu.make_async_remote_copy(
                    src_ref=src_ref.at[src],
                    dst_ref=dst_ref.at[dst],
                    send_sem=ssem.at[i],
                    recv_sem=rsem.at[i],
                    device_id=neighbour(d),
                    device_id_type=MESH,
                )
            )
        return copies

    def max_copies(axis):
        start = sum(dims[:axis])
        return [
            pltpu.make_async_remote_copy(
                src_ref=mx.at[axis],
                dst_ref=mx_parts.at[start + hop],
                send_sem=msend.at[start + hop],
                recv_sem=mrecv.at[start + hop],
                device_id=peer(axis, hop),
                device_id_type=MESH,
            )
            for hop in range(1, dims[axis])
        ]

    def start(copies):
        for c in copies:
            c.start()

    def wait(copies):
        for c in copies:
            c.wait()

    def max_result(axis):
        begin = sum(dims[:axis])
        total = mx[axis]
        for hop in range(1, dims[axis]):
            total = jnp.maximum(total, mx_parts[begin + hop])
        return total

    first_halo = halo_copies(f_in, 0, f_all, fsend, frecv)
    start(first_halo)

    def place(col, carry):
        x, y = col // by, col % by
        for z in range(bz):
            f_all[x + 1, y + 1, z + 1] = f_in[x, y, z]
        return carry

    lax.fori_loop(0, bx * by, place, 0)
    wait(first_halo)

    def centred(x, y, z):
        cx = x.astype(f32) - (0.5 * (bx + 1) + 0.5)
        cy = y.astype(f32) - (0.5 * (by + 1) + 0.5)
        cz = z - (0.5 * (bz + 1) + 0.5)
        shift = jnp.where(row == 0, cx, jnp.where(row == 1, cy, cz))
        pos = jnp.where(row < 3, f_all[x, y, z] + shift, 0.0)
        return pos, jnp.sum(pos * pos, axis=0, keepdims=True)

    def sources(col, carry):
        x, y = col // (by + 2), col % (by + 2)
        for z in range(bz + 2):
            pos, norm = centred(x, y, z)
            tile = jnp.where(row < 3, pos, jnp.where(row == 3, norm, jnp.where(row == 4, 1.0, 0.0)))
            hi, mid, lo = split3(tile)
            six = jnp.concatenate([hi, mid, hi, mid, lo, hi], axis=0)
            bt[x, y, z] = six.T.astype(bf16)
        return carry

    lax.fori_loop(0, (bx + 2) * (by + 2), sources, 0)

    def targets(col, carry):
        x, y = col // by, col % by
        for z in range(bz):
            pos, norm = centred(x + 1, y + 1, z + 1)
            tile = jnp.where(row < 3, -2.0 * pos, jnp.where(row == 3, 1.0, jnp.where(row == 4, norm, 0.0)))
            hi, mid, lo = split3(tile)
            at[x, y, z] = jnp.concatenate([hi, hi, mid, mid, hi, lo], axis=0).astype(bf16)
        return carry

    lax.fori_loop(0, bx * by, targets, 0)

    def spread(dist_sq):
        dist_sq = jnp.maximum(dist_sq, 1e-12)
        near = (1.0 - dist_sq * lax.rsqrt(dist_sq)).astype(bf16)
        near = jnp.maximum(near, jnp.zeros((), bf16))
        return near * near * near

    same = lax.broadcasted_iota(jnp.int32, (lanes, lanes), 0) == lax.broadcasted_iota(
        jnp.int32, (lanes, lanes), 1
    )

    def gen(step, carry):
        zp = step % (bz // 2)
        col = step // (bz // 2)
        x, y, z = col // by, col % by, zp * 2
        t = col * bz + z
        both = jnp.concatenate([at[x, y, z], at[x, y, z + 1]], axis=1)
        for c, (ex, ey) in enumerate(COLUMNS):
            for s in range(4):
                lo_t, hi_t = max(s - 2, 0), min(s, 1)
                a = both[:, lo_t * lanes : (hi_t + 1) * lanes]
                d2 = jnp.dot(bt[x + 1 + ex, y + 1 + ey, z + s], a, preferred_element_type=f32)
                for which in range(lo_t, hi_t + 1):
                    part = d2[:, (which - lo_t) * lanes : (which - lo_t + 1) * lanes]
                    if (ex, ey) == (0, 0) and s == which + 1:
                        part = jnp.where(same, 0.0, part)
                    k_all[t + which, c * 3 + s - which] = spread(part)
        return carry

    lax.fori_loop(0, bx * by * (bz // 2), gen, 0)

    def weigh(u_of):
        def body(col, carry):
            x, y = col // (by + 2), col % (by + 2)
            for z in range(bz + 2):
                tile = f_all[x, y, z]
                v, c = tile[3:4], tile[5:6]
                coef = jnp.where(row < 4, jnp.where(row % 2 == 0, v, v * c), 0.0)
                coef = coef * jnp.where(row < 2, u_of(x, y, z), 1.0)
                hi = coef.astype(bf16).astype(f32)
                w_all[x, y, z] = jnp.concatenate([hi, coef - hi], axis=0).astype(bf16)
            return carry

        lax.fori_loop(0, (bx + 2) * (by + 2), body, 0)

    def apply(u_of, emit, init):
        def body(col, carry):
            x, y = col // by, col % by
            for z in range(bz):
                w = jnp.concatenate(
                    [w_all[x + 1 + ex, y + 1 + ey, z + ez] for ex, ey in COLUMNS for ez in range(3)], axis=1
                )
                block_k = k_all[col * bz + z].reshape(27 * lanes, lanes)
                o = jnp.dot(w, block_k, preferred_element_type=f32)
                o = o[0:8] + o[8:16]
                u = u_of(x + 1, y + 1, z + 1)
                c = f_all[x + 1, y + 1, z + 1, 5:6]
                flow = c * (o[0:1] - u * o[2:3]) + (o[1:2] - u * o[3:4])
                carry = emit(carry, x, y, z, flow, c * o[2:3] + o[3:4])
            return carry

        return lax.fori_loop(0, bx * by, body, init)

    def u0_of(x, y, z):
        return f_all[x, y, z, 4:5]

    def u1_of(x, y, z):
        return u1[x, y, z]

    def u2_of(x, y, z):
        return u2[x, y, z]

    def emit0(carry, x, y, z, flow, rows):
        u1[x + 1, y + 1, z + 1] = flow
        return jnp.maximum(carry, rows * f_all[x + 1, y + 1, z + 1, 6:7])

    weigh(u0_of)
    largest = apply(u0_of, emit0, jnp.zeros((1, lanes), f32))
    mx[0] = jnp.broadcast_to(largest, (8, lanes))
    halo1 = halo_copies(u1, 1, u1, usend.at[0], urecv.at[0])
    max0 = max_copies(0)
    start(halo1)
    start(max0)
    wait(halo1)
    wait(max0)
    mx[1] = max_result(0)
    max1 = max_copies(1)
    start(max1)

    def emit1(carry, x, y, z, flow, rows):
        u2[x + 1, y + 1, z + 1] = flow
        return carry

    weigh(u1_of)
    apply(u1_of, emit1, 0)
    halo2 = halo_copies(u2, 1, u2, usend.at[1], urecv.at[1])
    start(halo2)
    wait(max1)
    mx[2] = max_result(1)
    max2 = max_copies(2)
    start(max2)
    wait(halo2)
    wait(max2)
    step = 2.0 / jnp.max(max_result(2)[0:1], axis=1, keepdims=True)

    def emit2(carry, x, y, z, f2, rows):
        u0 = f_all[x + 1, y + 1, z + 1, 4:5]
        f0, f1 = u1[x + 1, y + 1, z + 1], u2[x + 1, y + 1, z + 1]
        first = u0 + 2.0 / 15.0 * step * f0
        l_first = f0 + 2.0 / 15.0 * step * f1
        l_l_first = f1 + 2.0 / 15.0 * step * f2
        second = 1.5 * first - 0.5 * u0 + 0.6 * step * l_first - 0.4 * step * f0
        l_second = 1.5 * l_first - 0.5 * f0 + 0.6 * step * l_l_first - 0.4 * step * f1
        out[x, y, z] = (
            25.0 / 12.0 * second
            - 5.0 / 6.0 * first
            - 0.25 * u0
            + 5.0 / 6.0 * step * l_second
            - 5.0 / 9.0 * step * f0
        )
        return carry

    weigh(u2_of)
    apply(u2_of, emit2, 0)


def local(relative_placements, mass_per_density, opening_heat_level, bin_fill_counts):
    lanes = opening_heat_level.shape[-1]
    block = opening_heat_level.shape[:3]
    dims = tuple(lax.axis_size(a) for a in AXES)
    occupied = (
        jnp.arange(lanes, dtype=jnp.int32)[None, None, None, :] < bin_fill_counts[..., None]
    ).astype(f32)
    heat = opening_heat_level
    rows = [relative_placements[0], relative_placements[1], relative_placements[2]]
    rows += [mass_per_density * occupied, heat, heat * heat * jnp.sqrt(heat), occupied, jnp.zeros_like(heat)]
    fields = jnp.stack(rows, axis=3)
    outer = tuple(n + 2 for n in block)
    cells = block[0] * block[1] * block[2]
    vmem = pl.BlockSpec(memory_space=pltpu.VMEM)
    dma = pltpu.SemaphoreType.DMA
    n_dirs = len(DIRS)
    final = pl.pallas_call(
        functools.partial(kernel, dims, block),
        out_shape=jax.ShapeDtypeStruct(block + (1, lanes), f32),
        in_specs=[vmem],
        out_specs=vmem,
        scratch_shapes=[
            pltpu.VMEM(outer + (8, lanes), f32),
            pltpu.VMEM((cells, 27, lanes, lanes), bf16),
            pltpu.VMEM(outer + (lanes, 48), bf16),
            pltpu.VMEM(block + (48, lanes), bf16),
            pltpu.VMEM(outer + (16, lanes), bf16),
            pltpu.VMEM(outer + (1, lanes), f32),
            pltpu.VMEM(outer + (1, lanes), f32),
            pltpu.VMEM((3, 8, lanes), f32),
            pltpu.VMEM((sum(dims), 8, lanes), f32),
            dma((n_dirs,)),
            dma((n_dirs,)),
            dma((2, n_dirs)),
            dma((2, n_dirs)),
            dma((sum(dims),)),
            dma((sum(dims),)),
        ],
        compiler_params=pltpu.CompilerParams(
            collective_id=0, has_side_effects=True, vmem_limit_bytes=60 * 1024 * 1024
        ),
    )(fields)
    return final.reshape(heat.shape)


def solution(mesh):
    in_specs = (
        P(None, "gx", "gy", "gz", None),
        P("gx", "gy", "gz", None),
        P("gx", "gy", "gz", None),
        P("gx", "gy", "gz"),
    )
    out_specs = P("gx", "gy", "gz", None)
    return jax.shard_map(local, mesh=mesh, in_specs=in_specs, out_specs=out_specs, check_vma=False)
```

time: 388 us -> 73.7 us (0.19)
  other arithmetic: 190 us -> 0.93 us
  waiting for transfers between devices: 72 us -> 0 us
  Pallas kernels: 0 us -> 69.6 us
  starting transfers between devices: 39.9 us -> 0 us
  blocking collectives: 38.4 us -> 0 us
  local copies, waits for them, and re-layouts: 36.3 us -> 2.89 us
  loops' own time: 9.42 us -> 0 us
    reduce_sum x189 -> x0, other arithmetic: 178 us -> none  [visit(): jnp.sum(toward_target * spread, axis=2)]
    ppermute x36 -> x0, waiting for transfers between devices: 72 us -> none  [the longest x18 51.4 us: shifted(): return lax.ppermute(block, axis, route)]
    pallas_call x0 -> x1, Pallas kernels: none -> 69.6 us  [local(): pl.pallas_call(functools.partial(kernel, dims, block), out_shape=jax.Shap...]
    ppermute x36 -> x0, starting transfers between devices: 39.9 us -> none  [the longest x9 15.7 us: with_halo(): after = lax.ppermute(leading, axis, down)]
    pmax x1 -> x0, blocking collectives: 38.4 us -> none  [step_size(): largest = lax.pmax(jnp.max(row_sums), ('gx', 'gy', 'gz'))]
    dynamic_update_slice x270 -> x0, local copies, waits for them, and re-layouts: 33.7 us -> none  [the longest x243 30.3 us: visit(): lax.dynamic_update_slice(totals, window + returned.reshape((2, 1, 1, exte...]
    another operation x3 -> x0, loops' own time: 9.42 us -> none  [paired(): return lax.fori_loop(0, extent_x * extent_y, visit, totals)]
    add x302 -> x0, other arithmetic: 5.24 us -> none  [the longest x243 3.58 us: visit(): window + returned.reshape((2, 1, 1, extent_z, bin_dimensions))]
  transfers between devices with their start and end apart: 36 -> 0, of which waited for: 33 -> 0; matrix products, arithmetic and copies ran while one was open for 0% -> 0% of each run, Pallas kernels for 0% -> 0%
where the time goes in v1:
time: 73.7 us; the launch traced here: 73.5 us
  Pallas kernels  69.6 us (94%)
  local copies, waits for them, and re-layouts  2.89 us (4%)
  other arithmetic  0.93 us (1%)
    pallas_call x1, Pallas kernels, local(): pl.pallas_call(functools.partial(kernel, dims, block), out_shape=jax.Shap...  69.6 us
    unnamed x7, local copies, waits for them, and re-layouts  2 us

profile of v1, /device:TPU:0, one launch (start us, length us, event | category | flops | bytes accessed | tf_op | source)
XLA Modules:
  0.0 73.5 jit_solution(543987536089327392)
XLA Ops:
  0.0 0.0 copy-start
  0.0 0.0 copy-start.1
  0.0 0.8 %fusion = f32[3,3,4,128]{3,2,1,0:T(4,128)S(1)} fusion(f32[3,3,4,128]{3,2,1,0:T(4,128)} %param.5, s32[3,3,4]{2,1,0:T(4,128)} %param.7), kind=kLoop, calls=%fused_computation.3 | loop fusion | flops 9216 | bytes 37008 | tf_op jit(solution)/shard_map/mul | solution.py:284
  0.8 0.0 copy-done
  0.8 0.0 copy-start.2
  0.9 0.7 copy-done.2
  1.5 0.1 compare_convert_fusion
  1.6 0.0 copy-done.1
  1.7 0.9 %stack.16.f_in = f32[3,3,4,8,128]{4,3,2,1,0:T(8,128)} concatenate(f32[3,3,4,1,128]{4,3,2,1,0:T(1,128)S(1)} %bitcast.8, f32[3,3,4,1,128]{4,3,2,1,0:T(1,128)S(1)} %bitcast.9, f32[3,3,4,1,128]{4,3,2,1,0:T(1,128)S(1)} %bitcast.7, f32[3,3,4,1,128]{4,3,2,1,0:T(1,128)S(1)} %bitcast.12, f32[3,3,4,1,128]{4,3,2,1,0:T(1,128)S(1)} %bitcast.10, f32[3,3,4,1,128]{4,3,2,1,0:T(1,128)S(1)} %bitcast.11, ...), dimensions={3} | concatenate | bytes 294912 | tf_op jit(solution)/shard_map/stack | solution.py:285
  2.6 69.6 %shard_map.46 = f32[3,3,4,1,128]{4,3,2,1,0:T(1,128)} custom-call(f32[3,3,4,8,128]{4,3,2,1,0:T(8,128)} %stack.16.f_in), custom_call_target="tpu_custom_call" | custom-call | tf_op jit(solution)/shard_map/pallas_call | solution.py:291
  72.1 1.3 %copy.6 = f32[3,3,4,128]{3,2,1,0:T(4,128)} copy(f32[3,3,4,128]{3,2,1,0:T(4,128)} %bitcast.13) | data formatting | bytes 36864
  (3 shorter events, 0.0 us)
Async XLA Ops:
  0.0 0.8 %copy-start = (f32[3,3,4,128]{3,2,1,0:T(4,128)S(1)}, f32[3,3,4,128]{3,2,1,0:T(4,128)}, u32[]{:S(2)}) copy-start(f32[3,3,4,128]{3,2,1,0:T(4,128)} %param.6) | copy-start | bytes 55300
  0.0 1.6 %copy-start.1 = (f32[3,3,3,4,128]{4,3,2,1,0:T(4,128)S(1)}, f32[3,3,3,4,128]{4,3,2,1,0:T(4,128)}, u32[]{:S(2)}) copy-start(f32[3,3,3,4,128]{4,3,2,1,0:T(4,128)} %param.4) | copy-start | bytes 165892
  0.8 0.7 copy-start.2

commit v2 on v1

--- a/solution.py
+++ b/solution.py
@@ -114,27 +114,28 @@
         return carry
 
     lax.fori_loop(0, bx * by, place, 0)
-    wait(first_halo)
 
     def centred(x, y, z):
-        cx = x.astype(f32) - (0.5 * (bx + 1) + 0.5)
-        cy = y.astype(f32) - (0.5 * (by + 1) + 0.5)
+        cx = jnp.asarray(x, jnp.int32).astype(f32) - (0.5 * (bx + 1) + 0.5)
+        cy = jnp.asarray(y, jnp.int32).astype(f32) - (0.5 * (by + 1) + 0.5)
         cz = z - (0.5 * (bz + 1) + 0.5)
         shift = jnp.where(row == 0, cx, jnp.where(row == 1, cy, cz))
         pos = jnp.where(row < 3, f_all[x, y, z] + shift, 0.0)
         return pos, jnp.sum(pos * pos, axis=0, keepdims=True)
 
-    def sources(col, carry):
-        x, y = col // (by + 2), col % (by + 2)
-        for z in range(bz + 2):
-            pos, norm = centred(x, y, z)
-            tile = jnp.where(row < 3, pos, jnp.where(row == 3, norm, jnp.where(row == 4, 1.0, 0.0)))
-            hi, mid, lo = split3(tile)
-            six = jnp.concatenate([hi, mid, hi, mid, lo, hi], axis=0)
-            bt[x, y, z] = six.T.astype(bf16)
-        return carry
-
-    lax.fori_loop(0, (bx + 2) * (by + 2), sources, 0)
+    def source(x, y, z):
+        pos, norm = centred(x, y, z)
+        tile = jnp.where(row < 3, pos, jnp.where(row == 3, norm, jnp.where(row == 4, 1.0, 0.0)))
+        hi, mid, lo = split3(tile)
+        six = jnp.concatenate([hi, mid, hi, mid, lo, hi], axis=0)
+        bt[x, y, z] = six.T.astype(bf16)
+
+    def own_sources(col, carry):
+        for z in range(bz):
+            source(col // by + 1, col % by + 1, z + 1)
+        return carry
+
+    lax.fori_loop(0, bx * by, own_sources, 0)
 
     def targets(col, carry):
         x, y = col // by, col % by
@@ -157,25 +158,69 @@
         jnp.int32, (lanes, lanes), 1
     )
 
-    def gen(step, carry):
-        zp = step % (bz // 2)
-        col = step // (bz // 2)
-        x, y, z = col // by, col % by, zp * 2
-        t = col * bz + z
-        both = jnp.concatenate([at[x, y, z], at[x, y, z + 1]], axis=1)
-        for c, (ex, ey) in enumerate(COLUMNS):
+    def pairs(x, y, sx, sy, c, own, ends):
+        for zp in range(bz // 2):
+            z = 2 * zp
+            both = jnp.concatenate([at[x, y, z], at[x, y, z + 1]], axis=1)
             for s in range(4):
+                rim = (zp == 0 and s == 0) or (zp == bz // 2 - 1 and s == 3)
+                if rim != ends:
+                    continue
                 lo_t, hi_t = max(s - 2, 0), min(s, 1)
                 a = both[:, lo_t * lanes : (hi_t + 1) * lanes]
-                d2 = jnp.dot(bt[x + 1 + ex, y + 1 + ey, z + s], a, preferred_element_type=f32)
+                d2 = jnp.dot(bt[sx, sy, z + s], a, preferred_element_type=f32)
                 for which in range(lo_t, hi_t + 1):
                     part = d2[:, (which - lo_t) * lanes : (which - lo_t + 1) * lanes]
-                    if (ex, ey) == (0, 0) and s == which + 1:
+                    if own and s == which + 1:
                         part = jnp.where(same, 0.0, part)
-                    k_all[t + which, c * 3 + s - which] = spread(part)
-        return carry
-
-    lax.fori_loop(0, bx * by * (bz // 2), gen, 0)
+                    k_all[(x * by + y) * bz + z + which, c * 3 + s - which] = spread(part)
+
+    for c, (ex, ey) in enumerate(COLUMNS):
+        nx, ny = bx - abs(ex), by - abs(ey)
+        group = 3 if nx * ny % 3 == 0 else 2 if nx * ny % 2 == 0 else 1
+
+        def inner(step, carry, c=c, ex=ex, ey=ey, ny=ny, group=group):
+            for k in range(group):
+                i = step * group + k
+                x, y = max(0, -ex) + i // ny, max(0, -ey) + i % ny
+                pairs(x, y, x + 1 + ex, y + 1 + ey, c, (ex, ey) == (0, 0), False)
+            return carry
+
+        lax.fori_loop(0, nx * ny // group, inner, 0)
+
+    wait(first_halo)
+
+    def rim_sources(col, carry):
+        for z in range(bz + 2):
+            source(col // (by + 2), col % (by + 2), z)
+        return carry
+
+    lax.fori_loop(0, (bx + 2) * (by + 2), rim_sources, 0)
+
+    for side in (-1, 1):
+
+        def rim_x(e, carry, side=side):
+            x = bx - 1 if side == 1 else 0
+            for y in range(by):
+                pairs(x, y, x + 1 + side, y + e, (side + 1) * 3 + e, False, False)
+            return carry
+
+        def rim_y(e, carry, side=side):
+            y = by - 1 if side == 1 else 0
+            for x in range(bx):
+                pairs(x, y, x + e, y + 1 + side, e * 3 + side + 1, False, False)
+            return carry
+
+        lax.fori_loop(0, 3, rim_x, 0)
+        lax.fori_loop(0, 3, rim_y, 0)
+
+    def ends(col, carry):
+        x, y = col // by, col % by
+        for c, (ex, ey) in enumerate(COLUMNS):
+            pairs(x, y, x + 1 + ex, y + 1 + ey, c, False, True)
+        return carry
+
+    lax.fori_loop(0, bx * by, ends, 0)
 
     def weigh(u_of):
         def body(col, carry):

time: 73.7 us -> 71.3 us (0.967)
  Pallas kernels: 69.6 us -> 66.9 us
    pallas_call x1, Pallas kernels: 69.6 us -> 66.9 us  [local(): pl.pallas_call(functools.partial(kernel, dims, block), out_shape=jax.Shap...]
where the time goes in v2:
time: 71.3 us; the launch traced here: 70.8 us
  Pallas kernels  66.9 us (94%)
  local copies, waits for them, and re-layouts  2.89 us (4%)
  other arithmetic  0.93 us (1%)
    pallas_call x1, Pallas kernels, local(): pl.pallas_call(functools.partial(kernel, dims, block), out_shape=jax.Shap...  66.9 us
    unnamed x7, local copies, waits for them, and re-layouts  2 us

profile of v2, /device:TPU:0, one launch (start us, length us, event | category | flops | bytes accessed | tf_op | source)
XLA Modules:
  0.0 70.8 jit_solution(5192553049655295382)
XLA Ops:
  0.0 0.0 copy-start
  0.0 0.0 copy-start.1
  0.0 0.8 %fusion = f32[3,3,4,128]{3,2,1,0:T(4,128)S(1)} fusion(f32[3,3,4,128]{3,2,1,0:T(4,128)} %param.5, s32[3,3,4]{2,1,0:T(4,128)} %param.7), kind=kLoop, calls=%fused_computation.3 | loop fusion | flops 9216 | bytes 37008 | tf_op jit(solution)/shard_map/mul | solution.py:329
  0.8 0.0 copy-done
  0.8 0.0 copy-start.2
  0.9 0.7 copy-done.2
  1.5 0.1 compare_convert_fusion
  1.6 0.0 copy-done.1
  1.7 0.9 %stack.16.f_in = f32[3,3,4,8,128]{4,3,2,1,0:T(8,128)} concatenate(f32[3,3,4,1,128]{4,3,2,1,0:T(1,128)S(1)} %bitcast.8, f32[3,3,4,1,128]{4,3,2,1,0:T(1,128)S(1)} %bitcast.9, f32[3,3,4,1,128]{4,3,2,1,0:T(1,128)S(1)} %bitcast.7, f32[3,3,4,1,128]{4,3,2,1,0:T(1,128)S(1)} %bitcast.12, f32[3,3,4,1,128]{4,3,2,1,0:T(1,128)S(1)} %bitcast.10, f32[3,3,4,1,128]{4,3,2,1,0:T(1,128)S(1)} %bitcast.11, ...), dimensions={3} | concatenate | bytes 294912 | tf_op jit(solution)/shard_map/stack | solution.py:330
  2.6 66.9 %shard_map.46 = f32[3,3,4,1,128]{4,3,2,1,0:T(1,128)} custom-call(f32[3,3,4,8,128]{4,3,2,1,0:T(8,128)} %stack.16.f_in), custom_call_target="tpu_custom_call" | custom-call | tf_op jit(solution)/shard_map/pallas_call | solution.py:336
  69.4 1.3 %copy.6 = f32[3,3,4,128]{3,2,1,0:T(4,128)} copy(f32[3,3,4,128]{3,2,1,0:T(4,128)} %bitcast.13) | data formatting | bytes 36864
  (3 shorter events, 0.0 us)
Async XLA Ops:
  0.0 0.8 %copy-start = (f32[3,3,4,128]{3,2,1,0:T(4,128)S(1)}, f32[3,3,4,128]{3,2,1,0:T(4,128)}, u32[]{:S(2)}) copy-start(f32[3,3,4,128]{3,2,1,0:T(4,128)} %param.6) | copy-start | bytes 55300
  0.0 1.6 %copy-start.1 = (f32[3,3,3,4,128]{4,3,2,1,0:T(4,128)S(1)}, f32[3,3,3,4,128]{4,3,2,1,0:T(4,128)}, u32[]{:S(2)}) copy-start(f32[3,3,3,4,128]{4,3,2,1,0:T(4,128)} %param.4) | copy-start | bytes 165892
  0.8 0.7 copy-start.2
